TPU v7x, 512 devices: a whole 4x4x16 slice. The times are simulated.
512 devices in a mesh: dp: 16 (over x, z_hi, core), shard: 32 (over z_lo, y).
Axes of the slice: x: 4, y: 4, z: 16 (z_hi: 2, z_lo: 8; z = z_hi * 8 + z_lo), core: 2. Of those that a mesh axis runs over, the one named last changes fastest.
Arguments:
- tokens: bfloat16 [1024, 6144], P('dp', 'shard'), may hold values from -6 to 6
- cotangent: bfloat16 [1024, 6144], P('dp', 'shard'), may hold values from -12 to 12
- gate_proj: bfloat16 [2, 6144, 16384], P(None, 'dp', 'shard'), may hold values from -0.078125 to 0.078125
- up_proj: bfloat16 [2, 6144, 16384], P(None, 'dp', 'shard'), may hold values from -0.078125 to 0.078125
- down_proj: bfloat16 [2, 16384, 6144], P(None, 'shard', 'dp'), may hold values from -0.046875 to 0.046875
- slot_tokens: int32 [2, 256], P(None, 'dp'), may hold values from 0 to 63, as said below
- gate_weights: float32 [2, 256], P(None, 'dp'), may hold values from 0.1 to 1
- live_counts: int32 [2, 16], P(None, 'dp'), may hold values from 1 to 16, as said below
Outputs:
- grad_tokens: bfloat16 [1024, 6144], P('dp', 'shard')
- grad_gate_proj: bfloat16 [2, 6144, 16384], P(None, 'dp', 'shard')
- grad_up_proj: bfloat16 [2, 6144, 16384], P(None, 'dp', 'shard')
- grad_down_proj: bfloat16 [2, 16384, 6144], P(None, 'shard', 'dp')
Inputs may be any that keep to these rules, and one draw needn't show every extreme that they name: `slot_tokens`: for each expert and each index of dp, the 16 slots name 16 different tokens of that index. `live_counts`: the live slots of an expert at an index of dp are its first ones; 16 is reached at some index of every expert.
All inputs are finite; a program needn't handle non-finite values.
Results may differ from a plain program's by a relative error of at most 0.03.
Values may be sent and summed in bfloat16 or wider, within the bound.
No kernel may reach another device: no remote copies, remote signals or barrier semaphores. Data moves between devices by JAX's collectives and lax.ppermute only.
A program may use at most 64 MiB of HBM per device.

v0:
```python
import jax
import jax.numpy as jnp
from jax import lax
from jax.sharding import PartitionSpec as P


def gather_turned(arrays, axis, dims):
    turned = [jnp.moveaxis(a, dim, 0) for a, dim in zip(arrays, dims)]
    both = jnp.concatenate([t.reshape(len(t), -1) for t in turned], axis=1)
    result, at, outs = (lax.all_gather(both, axis, axis=0, tiled=True), 0, [])
    for t, dim in zip(turned, dims):
        slab = result[:, at : at + t[0].size].reshape(-1, *t.shape[1:])
        outs.append(jnp.moveaxis(slab, 0, dim))
        at += t[0].size
    return tuple(outs)


def in_one_piece(arrays, axis, split_dim, concat_dim, along):
    ends, at = ([], 0)
    for a in arrays[:-1]:
        at += a.shape[along]
        ends.append(at)
    both = jnp.concatenate(arrays, axis=along)
    return tuple(
        jnp.split(
            lax.all_to_all(both, axis, split_axis=split_dim, concat_axis=concat_dim, tiled=True),
            ends,
            axis=along,
        )
    )


def sent_together(arrays, axis, dim, along):
    ends, at = ([], 0)
    for a in arrays[:-1]:
        at += a.shape[along]
        ends.append(at)
    both = jnp.concatenate(arrays, axis=along)
    return tuple(
        jnp.split(lax.psum_scatter(both, axis, scatter_dimension=dim, tiled=True), ends, axis=along)
    )


def side_by_side(arrays, axis, dim, along):
    widths = [a.shape[along] for a in arrays]
    both = jnp.concatenate(arrays, axis=along)
    result = lax.all_gather(both, axis, axis=dim, tiled=True)
    return tuple(jnp.split(result, [sum(widths[:k]) for k in range(1, len(widths))], axis=along))


def cut_along(array, dim, count):
    before, after = (array.shape[:dim], array.shape[dim + 1 :])
    return jnp.moveaxis(array.reshape(*before, count, -1, *after), dim, 0)


def summed_on_arrival(array, axis, dim):
    count = lax.axis_size(axis)
    tiles = lax.all_to_all(cut_along(array, dim, count), axis, 0, 0, tiled=True)
    return jnp.sum(tiles.astype(jnp.float32), axis=0)


def slope_terms(gate_sum, up_sum, cot_hidden):
    sigmoid_part = jax.nn.sigmoid(gate_sum)
    grad_gate = (
        cot_hidden * up_sum * sigmoid_part * (1.0 + gate_sum * (1.0 - sigmoid_part))
    ).astype(jnp.bfloat16)
    grad_up = (cot_hidden * gate_sum * sigmoid_part).astype(jnp.bfloat16)
    return (grad_gate, grad_up)


def on_device(
    tokens, cotangent, gate_proj, up_proj, down_proj, slot_tokens, gate_weights, live_counts
):
    experts_here = slot_tokens.shape[0]
    slot_count = slot_tokens.shape[1]
    token_count = tokens.shape[0]
    position = lax.broadcasted_iota(jnp.int32, slot_tokens.shape, 1)
    alive_mask = (position < live_counts).astype(jnp.float32)
    picked = tokens[slot_tokens]
    weighted = (
        cotangent[slot_tokens].astype(jnp.float32) * (gate_weights * alive_mask)[:, :, None]
    ).astype(jnp.bfloat16)
    full_rows, full_cot = gather_turned((picked, weighted), "shard", (2, 2))
    spread = jnp.broadcast_to(live_counts[:, :, None], (experts_here, 1, lax.axis_size("dp")))
    block_rows, block_cot, heard = (
        *in_one_piece((full_rows, full_cot), "dp", 2, 1, 0),
        lax.all_to_all(spread, "dp", split_axis=2, concat_axis=1, tiled=True),
    )
    totals = jnp.sum(heard, axis=1).astype(jnp.float32)
    gate_part = jnp.einsum(
        "erd,edf->erf", block_rows, gate_proj, preferred_element_type=jnp.float32
    )
    up_part = jnp.einsum("erd,edf->erf", block_rows, up_proj, preferred_element_type=jnp.float32)
    cot_part = jnp.einsum("erd,efd->erf", block_cot, down_proj, preferred_element_type=jnp.float32)
    gate_sum, up_sum, cot_hidden = tuple(
        (
            part.astype(jnp.float32)
            for part in sent_together(
                (
                    gate_part.astype(jnp.bfloat16),
                    up_part.astype(jnp.bfloat16),
                    cot_part.astype(jnp.bfloat16),
                ),
                "dp",
                1,
                0,
            )
        )
    )
    hidden = (jax.nn.silu(gate_sum) * up_sum).astype(jnp.bfloat16)
    grad_gate, grad_up = slope_terms(gate_sum, up_sum, cot_hidden)
    hidden_all, gate_all, up_all = side_by_side((hidden, grad_gate, grad_up), "dp", 1, 0)
    scale_back = totals[:, :, None]
    grad_down_proj = (
        jnp.einsum("erf,erd->efd", hidden_all, block_cot, preferred_element_type=jnp.float32)
        / scale_back
    ).astype(jnp.bfloat16)
    grad_gate_proj = (
        jnp.einsum("erd,erf->edf", block_rows, gate_all, preferred_element_type=jnp.float32)
        / scale_back
    ).astype(jnp.bfloat16)
    grad_up_proj = (
        jnp.einsum("erd,erf->edf", block_rows, up_all, preferred_element_type=jnp.float32)
        / scale_back
    ).astype(jnp.bfloat16)
    back_term = (
        jnp.einsum("erf,edf->erd", gate_all, gate_proj, preferred_element_type=jnp.float32)
        + jnp.einsum("erf,edf->erd", up_all, up_proj, preferred_element_type=jnp.float32)
    ).astype(jnp.bfloat16)
    owned_rows = lax.all_to_all(back_term, "dp", split_axis=1, concat_axis=2, tiled=True)
    row_grads = summed_on_arrival(owned_rows.astype(jnp.float32).astype(jnp.bfloat16), "shard", 2)
    one_hot = (
        slot_tokens[:, :, None]
        == lax.broadcasted_iota(jnp.int32, (experts_here, slot_count, token_count), 2)
    ).astype(jnp.float32)
    grad_tokens = jnp.einsum("ert,erf->tf", one_hot, row_grads).astype(jnp.bfloat16)
    return (grad_tokens, grad_gate_proj, grad_up_proj, grad_down_proj)


def solution(mesh):
    in_specs = (
        P("dp", "shard"),
        P("dp", "shard"),
        P(None, "dp", "shard"),
        P(None, "dp", "shard"),
        P(None, "shard", "dp"),
        P(None, "dp"),
        P(None, "dp"),
        P(None, "dp"),
    )
    out_specs = (
        P("dp", "shard"),
        P(None, "dp", "shard"),
        P(None, "dp", "shard"),
        P(None, "shard", "dp"),
    )
    return jax.shard_map(
        on_device, mesh=mesh, in_specs=in_specs, out_specs=out_specs, check_vma=False
    )
```

profile of v0, /device:TPU:2, one launch (start us, length us, event | category | flops | bytes accessed | tf_op | source)
XLA Modules:
  0.0 493.9 jit_solution(5408034918978574355)
XLA Ops:
  8.1 1.4 gather_fusion.1
  9.4 1.4 gather_fusion
  11.6 133.1 %all-gather = bf16[32,192,64]{1,2,0:T(8,128)(2,1)S(1)} all-gather(bf16[1,192,64]{1,2,0:T(8,128)(2,1)S(1)} %maximum_bitcast_fusion), channel_id=1, replica_groups=mesh['dp'=16,'shard'=32] {'shard'}, dimensions={0}, use_global_device_ids=true | all-gather | bytes 811008 | tf_op jit(solution)/shard_map/all_gather | solution.py:10
  145.3 1.1 reshape.67
  146.6 6.2 %copy.40 = bf16[4,16,6144]{1,0,2:T(4,128)(2,1)} copy(bf16[4,16,6144]{2,1,0:T(8,128)(2,1)S(1)} %pad_maximum_fusion.1) | data formatting | bytes 1572864 | tf_op jit(solution)/shard_map/concatenate | solution.py:23
  152.8 9.3 %reshape.69 = bf16[16,2,12288]{2,1,0:T(2,128)(2,1)S(1)} reshape(bf16[6144,4,16]{2,1,0:T(4,128)(2,1)} %bitcast.53) | data formatting | bytes 1572864
  162.1 32.0 %all_to_all.44 = bf16[16,2,12288]{2,1,0:T(2,128)(2,1)S(1)} all-to-all(bf16[16,2,12288]{2,1,0:T(2,128)(2,1)S(1)} %reshape.69), channel_id=1, replica_groups=mesh['dp'=16,'shard'=32] {'dp'}, dimensions={0} | all-to-all | bytes 1572864 | tf_op jit(solution)/shard_map/all_to_all | solution.py:26
  194.1 5.6 %reshape.70 = bf16[6144,4,16]{2,1,0:T(4,128)(2,1)} reshape(bf16[16,2,12288]{2,1,0:T(2,128)(2,1)S(1)} %all_to_all.44) | data formatting | bytes 1572864
  199.8 6.6 %copy.53 = bf16[4,16,16,384]{3,2,1,0:T(8,128)(2,1)S(1)} copy(bf16[4,16,16,384]{1,0,3,2:T(4,128)(2,1)} %bitcast.54) | data formatting | bytes 1572864 | tf_op jit(solution)/shard_map/all_to_all | solution.py:26
  206.5 0.9 copy-done.2
  209.7 1.3 pad_maximum_fusion
  211.1 103.7 %reduce-scatter.2.cloned.1.call-done = bf16[6,16,512]{2,1,0:T(8,128)(2,1)} async-done(((bf16[6,256,512]{2,1,0:T(8,128)(2,1)}), bf16[6,16,512]{2,1,0:T(8,128)(2,1)}) %reduce-scatter.2.cloned.1.call-update) | async-done | bytes 98320 | tf_op jit(solution)/shard_map/reduce_scatter | solution.py:40
  316.3 77.8 %all-gather.3.cloned.1.call-done = bf16[6,256,512]{2,1,0:T(8,128)(2,1)} async-done(((bf16[6,16,512]{2,1,0:T(8,128)(2,1)}), bf16[6,256,512]{2,1,0:T(8,128)(2,1)}) %all-gather.3.cloned.1.call-update) | async-done | bytes 1572880 | tf_op jit(solution)/shard_map/all_gather | solution.py:47
  394.2 1.6 fusion.18
  396.7 20.0 %all_to_all.45 = bf16[2,256,384]{2,0,1:T(2,128)(2,1)S(1)} all-to-all(bf16[2,256,384]{2,0,1:T(2,128)(2,1)S(1)} %copy.44), channel_id=1, replica_groups=mesh['dp'=16,'shard'=32] {'dp'}, dimensions={1} | all-to-all | bytes 786432 | tf_op jit(solution)/shard_map/all_to_all | solution.py:130
  417.4 6.1 %all-to-all-start.3 = ((s32[2,1,16]{0,1,2:T(1,128)}), s32[2,1,16]{0,1,2:T(1,128)S(1)}, u32[]{:S(2)}, u32[]{:S(2)}) async-start(s32[2,1,16]{0,1,2:T(1,128)} %broadcast_in_dim.5), calls=%async_computation.4 | async-start | bytes 16384 | tf_op jit(solution)/shard_map/all_to_all | solution.py:87
  424.3 1.3 reshape.44
  425.7 1.1 copy.46
  426.8 10.1 %all-to-all-done.3 = s32[2,1,16]{0,1,2:T(1,128)S(1)} async-done(((s32[2,1,16]{0,1,2:T(1,128)}), s32[2,1,16]{0,1,2:T(1,128)S(1)}, u32[]{:S(2)}, u32[]{:S(2)}) %all-to-all-start.3) | async-done | bytes 160 | tf_op jit(solution)/shard_map/all_to_all | solution.py:87
  436.9 19.6 %all-to-all-start.2 = ((bf16[32,2,16,192]{3,2,1,0:T(8,128)(2,1)}), bf16[32,2,16,192]{3,2,1,0:T(8,128)(2,1)S(1)}, u32[]{:S(2)}, u32[]{:S(2)}) async-start(bf16[32,2,16,192]{3,2,1,0:T(8,128)(2,1)} %copy.46), calls=%async_computation.3 | async-start | bytes 1048576 | tf_op jit(solution)/shard_map/all_to_all | solution.py:58
  456.5 1.3 divide_convert_fusion.1
  457.8 1.3 divide_convert_fusion.2
  459.1 1.4 divide_convert_fusion
  460.5 25.6 %all-to-all-done.2 = bf16[32,2,16,192]{3,2,1,0:T(8,128)(2,1)S(1)} async-done(((bf16[32,2,16,192]{3,2,1,0:T(8,128)(2,1)}), bf16[32,2,16,192]{3,2,1,0:T(8,128)(2,1)S(1)}, u32[]{:S(2)}, u32[]{:S(2)}) %all-to-all-start.2) | async-done | bytes 393248 | tf_op jit(solution)/shard_map/all_to_all | solution.py:58
  (44 shorter events, 9.7 us)
Async XLA Ops:
  7.2 200.8 %copy-start = (bf16[2,384,512]{2,1,0:T(8,128)(2,1)S(1)}, bf16[2,384,512]{2,1,0:T(8,128)(2,1)}, u32[]{:S(2)}) copy-start(bf16[2,384,512]{2,1,0:T(8,128)(2,1)} %param.10) | copy-start | bytes 2359300
  7.2 307.6 %reduce-scatter.2.cloned.1.call-start = ((), (), s32[]{:S(2)}) async-start(), calls=%async_computation.5 | async-start | bytes 1671168 | tf_op jit(solution)/shard_map/reduce_scatter | solution.py:40
  206.4 1.1 copy-start.2
  207.9 1.3 copy-start.5
  208.5 0.7 copy-start.3
  211.0 183.1 %all-gather.3.cloned.1.call-start = ((), (), s32[]{:S(2)}) async-start(), calls=%async_computation.6 | async-start | bytes 1671168 | tf_op jit(solution)/shard_map/all_gather | solution.py:47
  394.2 1.6 copy-start.1
  396.3 20.5 %copy-start.6 = (s32[2,1]{0,1:T(1,128)S(1)}, s32[2,1]{0,1:T(1,128)}, u32[]{:S(2)}) copy-start(s32[2,1]{0,1:T(1,128)} %param.15) | copy-start | bytes 28
  417.4 19.5 %all-to-all-start.3 = ((s32[2,1,16]{0,1,2:T(1,128)}), s32[2,1,16]{0,1,2:T(1,128)S(1)}, u32[]{:S(2)}, u32[]{:S(2)}) async-start(s32[2,1,16]{0,1,2:T(1,128)} %broadcast_in_dim.5), calls=%async_computation.4 | async-start | bytes 16384 | tf_op jit(solution)/shard_map/all_to_all | solution.py:87
  436.9 49.2 %all-to-all-start.2 = ((bf16[32,2,16,192]{3,2,1,0:T(8,128)(2,1)}), bf16[32,2,16,192]{3,2,1,0:T(8,128)(2,1)S(1)}, u32[]{:S(2)}, u32[]{:S(2)}) async-start(bf16[32,2,16,192]{3,2,1,0:T(8,128)(2,1)} %copy.46), calls=%async_computation.3 | async-start | bytes 1048576 | tf_op jit(solution)/shard_map/all_to_all | solution.py:58
  457.8 1.3 copy-start.4
  459.1 27.1 %copy-start.7 = (s32[2,16]{1,0:T(2,128)S(1)}, s32[2,16]{1,0:T(2,128)}, u32[]{:S(2)}) copy-start(s32[2,16]{1,0:T(2,128)} %param.13) | copy-start | bytes 388
Sparse Core Ops, SparseCore 0:
  211.2 103.5 reduce-scatter.1
  318.7 75.3 all-gather.2
where the time goes:
time: 495 us; the launch traced here: 494 us
  waiting for transfers between devices  217 us (44%)
  blocking collectives  185 us (37%)
  local copies, waits for them, and re-layouts  38.6 us (8%)
  starting transfers between devices  25.7 us (5%)
  between operations  14.2 us (3%)
  matrix products  8.3 us (2%)
    all_gather x1, blocking collectives, gather_turned(): result, at, outs = (lax.all_gather(both, axis, axis=0, tiled=True), 0, [])  133 us
    reduce_scatter x1, waiting for transfers between devices, sent_together(): lax.psum_scatter(both, axis, scatter_dimension=dim, tiled=True)  104 us
    all_gather x1, waiting for transfers between devices, side_by_side(): result = lax.all_gather(both, axis, axis=dim, tiled=True)  77.8 us
    all_to_all x1, blocking collectives, in_one_piece(): lax.all_to_all(both, axis, split_axis=split_dim, concat_axis=concat_dim,...  32 us
    all_to_all x1, waiting for transfers between devices, summed_on_arrival(): tiles = lax.all_to_all(cut_along(array, dim, count), axis, 0, 0, tiled=True)  25.6 us
    all_to_all x1, blocking collectives, on_device(): lax.all_to_all(back_term, 'dp', split_axis=1, concat_axis=2, tiled=True)  20 us
    all_to_all x1, starting transfers between devices, summed_on_arrival(): tiles = lax.all_to_all(cut_along(array, dim, count), axis, 0, 0, tiled=True)  19.6 us
    unnamed x19, local copies, waits for them, and re-layouts  17.8 us
  transfers between devices with their start and end apart: 4, of which 4 were waited for; matrix products, arithmetic and copies ran while one was open for 1% of the time, Pallas kernels for 0%

commit v1 on v0

--- a/solution.py
+++ b/solution.py
@@ -7,7 +7,15 @@
 def gather_turned(arrays, axis, dims):
     turned = [jnp.moveaxis(a, dim, 0) for a, dim in zip(arrays, dims)]
     both = jnp.concatenate([t.reshape(len(t), -1) for t in turned], axis=1)
-    result, at, outs = (lax.all_gather(both, axis, axis=0, tiled=True), 0, [])
+
+    def detail_slabs(u_in):
+        crops = []
+        for _ in range(jax.lax.axis_size(axis)):
+            crops.append(u_in)
+        extra = jnp.stack(crops)
+        return jnp.concatenate(jax.lax.all_to_all(extra, axis, 0, 0), 0)
+
+    result, at, outs = (detail_slabs(both), 0, [])
     for t, dim in zip(turned, dims):
         slab = result[:, at : at + t[0].size].reshape(-1, *t.shape[1:])
         outs.append(jnp.moveaxis(slab, 0, dim))

time: 495 us -> 453 us (0.915)
  blocking collectives: 185 us -> 131 us
  waiting for transfers between devices: 217 us -> 229 us
    all_gather x1 -> x0, blocking collectives: 133 us -> none  [gather_turned(): result, at, outs = (lax.all_gather(both, axis, axis=0, tiled=True), 0, [])]
    all_to_all x0 -> x1, blocking collectives: none -> 67.2 us  [detail_slabs(): return jnp.concatenate(jax.lax.all_to_all(extra, axis, 0, 0), 0)]
    all_to_all x1, blocking collectives: 32 us -> 44 us  [in_one_piece(): lax.all_to_all(both, axis, split_axis=split_dim, concat_axis=concat_dim,...]
    reduce_scatter x1, waiting for transfers between devices: 104 us -> 116 us  [sent_together(): lax.psum_scatter(both, axis, scatter_dimension=dim, tiled=True)]
    unnamed x19 -> x18, local copies, waits for them, and re-layouts: 17.8 us -> 16.6 us
  transfers between devices with their start and end apart: 4 -> 4, of which waited for: 4 -> 4; matrix products, arithmetic and copies ran while one was open for 1% -> 2% of each run, Pallas kernels for 0% -> 0%
where the time goes in v1:
time: 453 us; the launch traced here: 452 us
  waiting for transfers between devices  229 us (51%)
  blocking collectives  131 us (29%)
  local copies, waits for them, and re-layouts  38.7 us (9%)
  starting transfers between devices  25.7 us (6%)
  between operations  14.3 us (3%)
  matrix products  8.32 us (2%)
  other arithmetic  4.63 us (1%)
    reduce_scatter x1, waiting for transfers between devices, sent_together(): lax.psum_scatter(both, axis, scatter_dimension=dim, tiled=True)  116 us
    all_gather x1, waiting for transfers between devices, side_by_side(): result = lax.all_gather(both, axis, axis=dim, tiled=True)  77.8 us
    all_to_all x1, blocking collectives, detail_slabs(): return jnp.concatenate(jax.lax.all_to_all(extra, axis, 0, 0), 0)  67.2 us
    all_to_all x1, blocking collectives, in_one_piece(): lax.all_to_all(both, axis, split_axis=split_dim, concat_axis=concat_dim,...  44 us
    all_to_all x1, waiting for transfers between devices, summed_on_arrival(): tiles = lax.all_to_all(cut_along(array, dim, count), axis, 0, 0, tiled=True)  25.6 us
    all_to_all x1, blocking collectives, on_device(): lax.all_to_all(back_term, 'dp', split_axis=1, concat_axis=2, tiled=True)  20 us
    all_to_all x1, starting transfers between devices, summed_on_arrival(): tiles = lax.all_to_all(cut_along(array, dim, count), axis, 0, 0, tiled=True)  19.6 us
    unnamed x18, local copies, waits for them, and re-layouts  16.6 us
  transfers between devices with their start and end apart: 4, of which 4 were waited for; matrix products, arithmetic and copies ran while one was open for 2% of the time, Pallas kernels for 0%

profile of v1, /device:TPU:2, one launch (start us, length us, event | category | flops | bytes accessed | tf_op | source)
XLA Modules:
  0.0 452.0 jit_solution(14560830559436735406)
XLA Ops:
  8.1 1.4 gather_fusion.1
  9.4 1.4 gather_fusion
  11.8 67.2 %all_to_all.49 = bf16[32,192,64]{1,2,0:T(8,128)(2,1)S(1)} all-to-all(bf16[32,192,64]{1,2,0:T(8,128)(2,1)S(1)} %stack.2), channel_id=1, replica_groups=mesh['dp'=16,'shard'=32] {'shard'}, dimensions={0} | all-to-all | bytes 1572864 | tf_op jit(solution)/shard_map/all_to_all | solution.py:16
  79.6 1.1 reshape.47
  80.9 6.2 %copy.34 = bf16[4,16,6144]{1,0,2:T(4,128)(2,1)} copy(bf16[4,16,6144]{2,1,0:T(8,128)(2,1)S(1)} %pad_maximum_fusion.1) | data formatting | bytes 1572864 | tf_op jit(solution)/shard_map/concatenate | solution.py:31
  87.1 9.3 %reshape.73 = bf16[16,2,12288]{2,1,0:T(2,128)(2,1)S(1)} reshape(bf16[6144,4,16]{2,1,0:T(4,128)(2,1)} %bitcast.51) | data formatting | bytes 1572864
  96.4 44.0 %all_to_all.50 = bf16[16,2,12288]{2,1,0:T(2,128)(2,1)S(1)} all-to-all(bf16[16,2,12288]{2,1,0:T(2,128)(2,1)S(1)} %reshape.73), channel_id=1, replica_groups=mesh['dp'=16,'shard'=32] {'dp'}, dimensions={0} | all-to-all | bytes 1572864 | tf_op jit(solution)/shard_map/all_to_all | solution.py:34
  140.4 5.6 %reshape.74 = bf16[6144,4,16]{2,1,0:T(4,128)(2,1)} reshape(bf16[16,2,12288]{2,1,0:T(2,128)(2,1)S(1)} %all_to_all.50) | data formatting | bytes 1572864
  146.0 6.6 %copy.47 = bf16[4,16,16,384]{3,2,1,0:T(8,128)(2,1)S(1)} copy(bf16[4,16,16,384]{1,0,3,2:T(4,128)(2,1)} %bitcast.52) | data formatting | bytes 1572864 | tf_op jit(solution)/shard_map/all_to_all | solution.py:34
  152.8 0.9 copy-done.2
  155.9 1.3 pad_maximum_fusion
  157.3 115.5 %reduce-scatter.2.cloned.1.call-done = bf16[6,16,512]{2,1,0:T(8,128)(2,1)} async-done(((bf16[6,256,512]{2,1,0:T(8,128)(2,1)}), bf16[6,16,512]{2,1,0:T(8,128)(2,1)}) %reduce-scatter.2.cloned.1.call-update) | async-done | bytes 98320 | tf_op jit(solution)/shard_map/reduce_scatter | solution.py:48
  274.4 77.8 %all-gather.2.cloned.1.call-done = bf16[6,256,512]{2,1,0:T(8,128)(2,1)} async-done(((bf16[6,16,512]{2,1,0:T(8,128)(2,1)}), bf16[6,256,512]{2,1,0:T(8,128)(2,1)}) %all-gather.2.cloned.1.call-update) | async-done | bytes 1572880 | tf_op jit(solution)/shard_map/all_gather | solution.py:55
  352.2 1.6 fusion.18
  354.8 20.0 %all_to_all.51 = bf16[2,256,384]{2,0,1:T(2,128)(2,1)S(1)} all-to-all(bf16[2,256,384]{2,0,1:T(2,128)(2,1)S(1)} %copy.38), channel_id=1, replica_groups=mesh['dp'=16,'shard'=32] {'dp'}, dimensions={1} | all-to-all | bytes 786432 | tf_op jit(solution)/shard_map/all_to_all | solution.py:138
  375.4 6.1 %all-to-all-start.4 = ((s32[2,1,16]{0,1,2:T(1,128)}), s32[2,1,16]{0,1,2:T(1,128)S(1)}, u32[]{:S(2)}, u32[]{:S(2)}) async-start(s32[2,1,16]{0,1,2:T(1,128)} %broadcast_in_dim.5), calls=%async_computation.5 | async-start | bytes 16384 | tf_op jit(solution)/shard_map/all_to_all | solution.py:95
  382.4 1.3 reshape.50
  383.7 1.1 copy.40
  384.8 10.1 %all-to-all-done.4 = s32[2,1,16]{0,1,2:T(1,128)S(1)} async-done(((s32[2,1,16]{0,1,2:T(1,128)}), s32[2,1,16]{0,1,2:T(1,128)S(1)}, u32[]{:S(2)}, u32[]{:S(2)}) %all-to-all-start.4) | async-done | bytes 160 | tf_op jit(solution)/shard_map/all_to_all | solution.py:95
  394.9 19.6 %all-to-all-start.3 = ((bf16[32,2,16,192]{3,2,1,0:T(8,128)(2,1)}), bf16[32,2,16,192]{3,2,1,0:T(8,128)(2,1)S(1)}, u32[]{:S(2)}, u32[]{:S(2)}) async-start(bf16[32,2,16,192]{3,2,1,0:T(8,128)(2,1)} %copy.40), calls=%async_computation.4 | async-start | bytes 1048576 | tf_op jit(solution)/shard_map/all_to_all | solution.py:66
  414.5 1.3 divide_convert_fusion.1
  415.8 1.3 divide_convert_fusion.2
  417.1 1.4 divide_convert_fusion
  418.6 25.6 %all-to-all-done.3 = bf16[32,2,16,192]{3,2,1,0:T(8,128)(2,1)S(1)} async-done(((bf16[32,2,16,192]{3,2,1,0:T(8,128)(2,1)}), bf16[32,2,16,192]{3,2,1,0:T(8,128)(2,1)S(1)}, u32[]{:S(2)}, u32[]{:S(2)}) %all-to-all-start.3) | async-done | bytes 393248 | tf_op jit(solution)/shard_map/all_to_all | solution.py:66
  (45 shorter events, 9.8 us)
Async XLA Ops:
  7.2 147.0 %copy-start = (bf16[2,384,512]{2,1,0:T(8,128)(2,1)S(1)}, bf16[2,384,512]{2,1,0:T(8,128)(2,1)}, u32[]{:S(2)}) copy-start(bf16[2,384,512]{2,1,0:T(8,128)(2,1)} %param.10) | copy-start | bytes 2359300
  7.2 265.7 %reduce-scatter.2.cloned.1.call-start = ((), (), s32[]{:S(2)}) async-start(), calls=%async_computation.6 | async-start | bytes 1671168 | tf_op jit(solution)/shard_map/reduce_scatter | solution.py:48
  152.6 1.1 copy-start.2
  154.2 1.3 copy-start.5
  154.7 0.7 copy-start.3
  157.3 194.9 %all-gather.2.cloned.1.call-start = ((), (), s32[]{:S(2)}) async-start(), calls=%async_computation.7 | async-start | bytes 1671168 | tf_op jit(solution)/shard_map/all_gather | solution.py:55
  352.2 1.6 copy-start.1
  354.3 20.5 %copy-start.6 = (s32[2,1]{0,1:T(1,128)S(1)}, s32[2,1]{0,1:T(1,128)}, u32[]{:S(2)}) copy-start(s32[2,1]{0,1:T(1,128)} %param.15) | copy-start | bytes 28
  375.4 19.5 %all-to-all-start.4 = ((s32[2,1,16]{0,1,2:T(1,128)}), s32[2,1,16]{0,1,2:T(1,128)S(1)}, u32[]{:S(2)}, u32[]{:S(2)}) async-start(s32[2,1,16]{0,1,2:T(1,128)} %broadcast_in_dim.5), calls=%async_computation.5 | async-start | bytes 16384 | tf_op jit(solution)/shard_map/all_to_all | solution.py:95
  394.9 49.2 %all-to-all-start.3 = ((bf16[32,2,16,192]{3,2,1,0:T(8,128)(2,1)}), bf16[32,2,16,192]{3,2,1,0:T(8,128)(2,1)S(1)}, u32[]{:S(2)}, u32[]{:S(2)}) async-start(bf16[32,2,16,192]{3,2,1,0:T(8,128)(2,1)} %copy.40), calls=%async_computation.4 | async-start | bytes 1048576 | tf_op jit(solution)/shard_map/all_to_all | solution.py:66
  415.8 1.3 copy-start.4
  417.1 27.1 %copy-start.7 = (s32[2,16]{1,0:T(2,128)S(1)}, s32[2,16]{1,0:T(2,128)}, u32[]{:S(2)}) copy-start(s32[2,16]{1,0:T(2,128)} %param.13) | copy-start | bytes 388
Sparse Core Ops, SparseCore 0:
  157.4 115.4 reduce-scatter.1
  276.8 75.3 all-gather.1
